TPU v7x, 32 devices: a whole 2x2x4 slice. The times are simulated.
32 devices in a mesh: grp: 2 (over y), seq: 8 (over z, x), head: 2 (over core).
Axes of the slice: x: 2, y: 2, z: 4, core: 2. Of those that a mesh axis runs over, the one named last changes fastest.
Arguments:
- queries: bfloat16 [6144, 768], P(('grp', 'seq'), 'head'), parts along dimension 0, may hold values from -6 to 6
- key_rows: bfloat16 [6144, 768], P(('grp', 'seq'), 'head'), parts along dimension 0, may hold values from -6 to 6
- value_rows: bfloat16 [6144, 768], P(('grp', 'seq'), 'head'), parts along dimension 0, may hold values from -6 to 6
- gate_input: bfloat16 [6144, 768], P(('grp', 'seq'), 'head'), parts along dimension 0, may hold values from -6 to 6
- norm_gain: float32 [768], P('head'), may hold values from 0.5 to 1.5
Outputs:
- retained: bfloat16 [6144, 768], P(('grp', 'seq'), 'head'), parts along dimension 0
- final_state: float32 [256, 6, 128], P(('grp', 'seq'), 'head'), parts along dimension 0
There are 2 independent parts, one for each index of `grp`. A program takes and returns all parts, laid end to end along the dimension named above; an argument that names none is the same for every part. Nothing has to cross between parts.
All inputs are finite; a program needn't handle non-finite values.
Results may differ from a plain program's by a relative error of at most 0.0056.
Values sent between devices are 32-bit elements; how exact they have to be, the bound alone decides.
A program may use at most 128 MiB of HBM per device.

v0:
```python
import jax
import jax.numpy as jnp
from jax import lax
from jax.sharding import PartitionSpec as P

ALL_HEADS = 10
HEADS = 6
DH = 128


def entering(shard, axis, combine, identity):
    peers, mine = (lax.axis_size(axis), lax.axis_index(axis))
    everything = jax.tree.map(lambda part: lax.all_gather(part, axis), shard)
    start = jax.tree.map(
        lambda part, zero: jnp.broadcast_to(jnp.asarray(zero, part.dtype), part.shape),
        shard,
        identity,
    )

    def hop(k, before):
        reached = k < mine
        new = combine(before, jax.tree.map(lambda part: part[k], everything))
        return jax.tree.map(lambda a, b: jnp.where(reached, a, b), new, before)

    return lax.fori_loop(0, peers, hop, start)


def combine(earlier, latter):
    return (earlier[0] * latter[0], latter[0][None, :, None] * earlier[1] + latter[1])


def body(queries, key_rows, value_rows, gate_input, norm_gain):
    tokens = queries.shape[0]
    local_heads = queries.shape[1] // DH
    key_scale = DH ** (-0.5)
    head_ids = (
        ALL_HEADS
        - HEADS
        + lax.axis_index("head") * local_heads
        + jnp.arange(local_heads, dtype=jnp.int32)
    ).astype(jnp.float32)
    log_decay = jnp.log1p(-jnp.exp2(-5.0 - head_ids))
    split_shape = (tokens, local_heads, DH)
    query_split = queries.reshape(split_shape)
    key_split = key_rows.reshape(split_shape)
    value_split = value_rows.reshape(split_shape)
    places = jnp.arange(tokens, dtype=jnp.float32)
    offsets = places[:, None] - places[None, :]
    causal = offsets >= 0
    decays = jnp.where(
        causal[None], jnp.exp(jnp.where(causal, offsets, 0.0)[None] * log_decay[:, None, None]), 0.0
    )
    tail_decay = jnp.exp((tokens - 1 - places)[:, None] * log_decay[None, :])
    keys_decayed = (key_split.astype(jnp.float32) * key_scale * tail_decay[:, :, None]).astype(
        jnp.bfloat16
    )
    local_state = jnp.einsum(
        "shi,shj->ihj", keys_decayed, value_split, preferred_element_type=jnp.float32
    )
    block_decay = jnp.exp(tokens * log_decay)
    identity = (jnp.ones_like(block_decay), jnp.zeros_like(local_state))
    prefix_decay, carried = entering((block_decay, local_state), "seq", combine, identity)
    scores = (
        jnp.einsum("thd,shd->hts", query_split, key_split, preferred_element_type=jnp.float32)
        * key_scale
    )
    weights = (scores * decays).astype(jnp.bfloat16)
    inner_term = jnp.einsum(
        "hts,shd->thd", weights, value_split, preferred_element_type=jnp.float32
    )
    lead_decay = jnp.exp((places + 1)[:, None] * log_decay[None, :])
    outer_term = (
        jnp.einsum(
            "thi,ihj->thj",
            query_split,
            carried.astype(jnp.bfloat16),
            preferred_element_type=jnp.float32,
        )
        * lead_decay[:, :, None]
    )
    mixture = inner_term + outer_term
    centred = mixture - jnp.mean(mixture, axis=-1, keepdims=True)
    variance = jnp.mean(centred * centred, axis=-1, keepdims=True)
    normed = centred * lax.rsqrt(variance + 1e-05) * norm_gain.reshape(local_heads, DH)
    gated = normed * jax.nn.silu(gate_input.reshape(split_shape).astype(jnp.float32))
    result = gated.astype(jnp.bfloat16).reshape(tokens, local_heads * DH)
    ahead = (lax.axis_size("seq") - 1 - lax.axis_index("seq")).astype(jnp.float32)
    scaled_terms = jnp.exp(ahead * tokens * log_decay)[None, :, None] * local_state
    final_state = lax.psum_scatter(scaled_terms, "seq", scatter_dimension=0, tiled=True)
    return (result, final_state)


def solution(mesh):
    return jax.shard_map(
        body,
        mesh=mesh,
        in_specs=(
            P(("grp", "seq"), "head"),
            P(("grp", "seq"), "head"),
            P(("grp", "seq"), "head"),
            P(("grp", "seq"), "head"),
            P("head"),
        ),
        out_specs=(P(("grp", "seq"), "head"), P(("grp", "seq"), "head", None)),
        check_vma=False,
    )
```

profile of v0, /device:TPU:0, one launch (start us, length us, event | category | flops | bytes accessed | tf_op | source)
XLA Modules:
  0.0 129.0 jit_solution(3476014860007139148)
XLA Ops:
  7.2 1.2 copy.29
  8.5 1.2 copy.32
  9.8 1.0 broadcast_multiply_fusion
  10.9 0.7 reduce-scatter.2.cloned.1.call-update
  11.6 0.1 fusion.11
  11.8 0.1 fusion.12
  11.9 22.4 %all-gather.1 = f32[8,1,3]{2,1,0:T(1,128)S(1)} all-gather(f32[1,1,3]{2,1,0:T(1,128)S(1)} %exponential_bitcast_fusion), channel_id=1, replica_groups=mesh['grp'=2,'seq'=8,'head'=2] {'seq'}, dimensions={0}, use_global_device_ids=true | all-gather | bytes 108 | tf_op jit(solution)/shard_map/all_gather | solution.py:13
  34.3 0.2 copy.28
  34.5 0.2 copy.39
  34.7 23.2 %all-gather.4.cloned.1.call-done = f32[1024,3,128]{2,0,1:T(8,128)} async-done(((f32[128,3,128]{2,0,1:T(8,128)}), f32[1024,3,128]{2,0,1:T(8,128)}) %all-gather.4.cloned.1.call-update) | async-done | bytes 1572880 | tf_op jit(solution)/shard_map/all_gather | solution.py:13
  57.9 9.9 %while.14 = (s32[]{:T(128)}, f32[128,3,128]{2,1,0:T(4,128)S(1)}, s32[]{:T(128)}, f32[8,3]{1,0:T(8,128)S(1)}, f32[8,128,3,128]{3,1,0,2:T(8,128)}, /*index=5*/s32[]{:T(128)}, s32[]{:T(128)}) while((s32[]{:T(128)}, f32[128,3,128]{2,1,0:T(4,128)S(1)}, s32[]{:T(128)}, f32[8,3]{1,0:T(8,128)S(1)}, f32[8,128,3,128]{3,1,0,2:T(8,128)}, ...), condition=%wide.region_1.2_spmd.clone, body=%wide.region_0.1_spmd.clone.sunk | while | flops 196612 | bytes 983181 | solution.py:25
  57.9 0.9 constant_dynamic-slice_fusion.2
  58.9 0.2 fusion.24
  59.1 0.9 constant_dynamic-slice_fusion.2
  60.1 0.2 fusion.24
  60.4 0.9 constant_dynamic-slice_fusion.2
  61.4 0.2 fusion.24
  61.6 0.9 constant_dynamic-slice_fusion.2
  62.6 0.2 fusion.24
  62.8 0.9 constant_dynamic-slice_fusion.2
  63.8 0.2 fusion.24
  64.1 0.9 constant_dynamic-slice_fusion.2
  65.1 0.2 fusion.24
  65.3 0.9 constant_dynamic-slice_fusion.2
  66.3 0.2 fusion.24
  66.5 1.0 constant_dynamic-slice_fusion.2
  67.5 0.2 fusion.24
  67.8 0.3 fusion.5
  68.1 1.0 fusion.17
  69.2 0.2 multiply_convert_fusion.1
  69.5 0.9 copy.40
  70.4 51.8 %reduce-scatter.2.cloned.1.call-done = f32[16,3,128]{2,0,1:T(8,128)} async-done(((f32[128,3,128]{2,0,1:T(8,128)}), f32[16,3,128]{2,0,1:T(8,128)}) %reduce-scatter.2.cloned.1.call-update) | async-done | bytes 24592 | tf_op jit(solution)/shard_map/reduce_scatter | solution.py:89
  (26 shorter events, 0.5 us)
Async XLA Ops:
  7.2 50.8 %all-gather.4.cloned.1.call-start = ((), (), s32[]{:S(2)}) async-start(), calls=%async_computation.2 | async-start | bytes 1769472 | tf_op jit(solution)/shard_map/all_gather | solution.py:13
  7.2 27.1 %copy-start.1 = (bf16[384,384]{1,0:T(8,128)(2,1)S(1)}, bf16[384,384]{1,0:T(8,128)(2,1)}, u32[]{:S(2)}) copy-start(bf16[384,384]{1,0:T(8,128)(2,1)} %param.7) | copy-start | bytes 884740
  8.5 26.1 %copy-start = (bf16[384,384]{1,0:T(8,128)(2,1)S(1)}, bf16[384,384]{1,0:T(8,128)(2,1)}, u32[]{:S(2)}) copy-start(bf16[384,384]{1,0:T(8,128)(2,1)} %param.10) | copy-start | bytes 884740
  10.9 111.3 %reduce-scatter.2.cloned.1.call-start = ((), (), s32[]{:S(2)}) async-start(), calls=%async_computation.1 | async-start | bytes 221184 | tf_op jit(solution)/shard_map/reduce_scatter | solution.py:89
  68.1 1.1 copy-start.2
Sparse Core Ops, SparseCore 0:
  11.0 46.8 all-gather.3
  61.8 60.3 reduce-scatter.1
where the time goes:
time: 129 us
  waiting for transfers between devices  75.7 us (59%)
  blocking collectives  22.4 us (17%)
  between operations  14.2 us (11%)
  local copies, waits for them, and re-layouts  11.4 us (9%)
  other arithmetic  2.76 us (2%)
  matrix products  2.27 us (2%)
    reduce_scatter x1, waiting for transfers between devices, body(): lax.psum_scatter(scaled_terms, 'seq', scatter_dimension=0, tiled=True)  51.8 us
    all_gather x1, waiting for transfers between devices, entering(): everything = jax.tree.map(lambda part: lax.all_gather(part, axis), shard)  23.2 us
    all_gather x1, blocking collectives, entering(): everything = jax.tree.map(lambda part: lax.all_gather(part, axis), shard)  22.4 us
    dynamic_slice x8, local copies, waits for them, and re-layouts, hop(): new = combine(before, jax.tree.map(lambda part: part[k], everything))  7.58 us
    unnamed x10, local copies, waits for them, and re-layouts  3.56 us
  transfers between devices with their start and end apart: 2, of which 2 were waited for; matrix products, arithmetic and copies ran while one was open for 10% of the time, Pallas kernels for 0%

commit v1 on v0

v1 whole, which is shorter than its diff:
```python
import functools
import math

import jax
import jax.numpy as jnp
from jax import lax
from jax.experimental import pallas as pl
from jax.experimental.pallas import tpu as pltpu
from jax.sharding import PartitionSpec as P

ALL_HEADS = 10
HEADS = 6
DH = 128
MESH = pl.DeviceIdType.MESH
LOGS = [math.log1p(-(2.0 ** (-5 - (ALL_HEADS - HEADS + h)))) for h in range(HEADS)]


def flip(me, step, n):
    if n & (n - 1):
        return lax.rem(me + step, n)
    other = me
    bit = 1
    while bit < n:
        if step & bit:
            other = other + bit - 2 * bit * lax.rem(lax.div(me, bit), 2)
        bit *= 2
    return other


def each_peer(me, n, act):
    if n <= 16:
        for step in range(n - 1, 0, -1):
            act(flip(me, step, n))
    else:

        def go(step, carry):
            act(lax.rem(me + step, n))
            return carry

        lax.fori_loop(1, n, go, 0)


def kernel(
    n, heads, groups,
    q_hbm, k_hbm, v_hbm, g_hbm, gain_ref,
    out_ref, fin_ref,
    q, k, v, g, inner, gate, state, got, before, carried,
    load, send1, recv1, send2, recv2,
):
    me = lax.axis_index("seq")
    side = lax.axis_index("head")
    tokens = q.shape[0]
    rows = DH // n
    scale = DH ** (-0.5)

    loads = [
        pltpu.make_async_copy(src, dst, load.at[i])
        for i, (src, dst) in enumerate(((k_hbm, k), (v_hbm, v), (q_hbm, q), (g_hbm, g)))
    ]
    for copy in loads:
        copy.start()

    barrier = pltpu.get_barrier_semaphore()
    each_peer(
        me, n,
        lambda peer: pl.semaphore_signal(
            barrier, inc=1, device_id={"seq": peer}, device_id_type=MESH
        ),
    )

    logs = []
    for h in range(heads):
        log = jnp.float32(LOGS[h])
        for s in range(1, groups):
            log = jnp.where(side == s, jnp.float32(LOGS[s * heads + h]), log)
        logs.append(log)

    place = lax.broadcasted_iota(jnp.int32, (tokens, DH), 0).astype(jnp.float32)

    def cols(h):
        return slice(h * DH, (h + 1) * DH)

    def send(source, target, slot_of, sems, h):
        def act(peer):
            pltpu.make_async_remote_copy(
                src_ref=source.at[h, peer],
                dst_ref=target.at[h, me],
                send_sem=sems[0].at[h],
                recv_sem=sems[1].at[h],
                device_id={"seq": peer},
                device_id_type=MESH,
            ).start()

        each_peer(me, n, act)

    def drain(buffer, sem, h):
        piece = buffer.at[h, pl.ds(0, n - 1)]
        pltpu.make_async_copy(piece, piece, sem.at[h]).wait()

    loads[0].wait()
    loads[1].wait()
    for h in range(heads):
        tail = jnp.exp((tokens - 1 - place) * logs[h])
        kd = (k[:, cols(h)].astype(jnp.float32) * scale * tail).astype(jnp.bfloat16)
        local = lax.dot_general(
            kd, v[:, cols(h)], (((0,), (0,)), ((), ())), preferred_element_type=jnp.float32
        )
        state[h] = local.reshape(n, rows, DH)
    pl.semaphore_wait(barrier, n - 1)
    for h in range(heads):
        send(state, got, me, (send1, recv1), h)
        got[h, me] = state[h, me]

    loads[2].wait()
    offsets = (
        lax.broadcasted_iota(jnp.int32, (tokens, tokens), 0)
        - lax.broadcasted_iota(jnp.int32, (tokens, tokens), 1)
    ).astype(jnp.float32)
    causal = offsets >= 0
    for h in range(heads):
        scores = lax.dot_general(
            q[:, cols(h)], k[:, cols(h)], (((1,), (1,)), ((), ())),
            preferred_element_type=jnp.float32,
        ) * scale
        decays = jnp.where(causal, jnp.exp(jnp.where(causal, offsets, 0.0) * logs[h]), 0.0)
        weights = (scores * decays).astype(jnp.bfloat16)
        inner[h] = jnp.dot(weights, v[:, cols(h)], preferred_element_type=jnp.float32)
    loads[3].wait()
    for h in range(heads):
        u = g[:, cols(h)].astype(jnp.float32)
        gate[h] = u / (1.0 + jnp.exp(-u)) * gain_ref[:, cols(h)]

    for h in range(heads):
        drain(got, recv1, h)
        block_decay = jnp.exp(jnp.full((rows, DH), tokens, jnp.float32) * logs[h])

        def hop(b, total):
            before[h, b] = total
            return block_decay * total + got[h, b]

        total = jnp.zeros((rows, DH), jnp.float32)
        if n <= 16:
            for b in range(n):
                total = hop(b, total)
        else:
            total = lax.fori_loop(0, n, hop, total)
        send(before, carried, me, (send2, recv2), h)
        carried[h, me] = before[h, me]
        fin_ref[h] = total

    for h in range(heads):
        lead = jnp.exp((place + 1.0) * logs[h])
        drain(carried, recv2, h)
        low = carried[h].reshape(DH, DH).astype(jnp.bfloat16)
        outer = jnp.dot(q[:, cols(h)], low, preferred_element_type=jnp.float32)
        mixture = inner[h] + outer * lead
        centred = mixture - jnp.mean(mixture, axis=-1, keepdims=True)
        variance = jnp.mean(centred * centred, axis=-1, keepdims=True)
        normed = centred * lax.rsqrt(variance + 1e-05)
        out_ref[:, cols(h)] = (normed * gate[h]).astype(jnp.bfloat16)

    for h in range(heads):
        drain(state, send1, h)
        drain(before, send2, h)


def solution(mesh):
    n = mesh.shape["seq"]
    groups = mesh.shape["head"]

    def body(queries, key_rows, value_rows, gate_input, norm_gain):
        tokens, width = queries.shape
        heads = width // DH
        rows = DH // n
        slab = pltpu.VMEM((heads, n, rows, DH), jnp.float32)
        wide = pltpu.VMEM((tokens, width), jnp.bfloat16)
        tall = pltpu.VMEM((heads, tokens, DH), jnp.float32)
        anywhere = pl.BlockSpec(memory_space=pl.ANY)
        vmem = pl.BlockSpec(memory_space=pltpu.VMEM)
        retained, final = pl.pallas_call(
            functools.partial(kernel, n, heads, groups),
            out_shape=(
                jax.ShapeDtypeStruct((tokens, width), jnp.bfloat16),
                jax.ShapeDtypeStruct((heads, rows, DH), jnp.float32),
            ),
            in_specs=[anywhere] * 4 + [vmem],
            out_specs=(vmem, vmem),
            scratch_shapes=[wide] * 4 + [tall] * 2 + [slab] * 4
            + [pltpu.SemaphoreType.DMA((4,))] + [pltpu.SemaphoreType.DMA((heads,))] * 4,
            compiler_params=pltpu.CompilerParams(collective_id=0, has_side_effects=True),
            name="retention",
        )(queries, key_rows, value_rows, gate_input, norm_gain.reshape(1, width))
        return retained, final.transpose(1, 0, 2)

    return jax.shard_map(
        body,
        mesh=mesh,
        in_specs=(P(("grp", "seq"), "head"),) * 4 + (P("head"),),
        out_specs=(P(("grp", "seq"), "head"), P(("grp", "seq"), "head", None)),
        check_vma=False,
    )
```

time: 129 us -> 23.2 us (0.18)
  waiting for transfers between devices: 75.7 us -> 0 us
  blocking collectives: 22.4 us -> 0 us
  Pallas kernels: 0 us -> 18.7 us
  between operations: 14.2 us -> 0.65 us
  local copies, waits for them, and re-layouts: 11.4 us -> 3.57 us
  other arithmetic: 2.76 us -> 0 us
  matrix products: 2.27 us -> 0 us
    reduce_scatter x1 -> x0, waiting for transfers between devices: 51.8 us -> none  [body(): lax.psum_scatter(scaled_terms, 'seq', scatter_dimension=0, tiled=True)]
    all_gather x1 -> x0, waiting for transfers between devices: 23.2 us -> none  [entering(): everything = jax.tree.map(lambda part: lax.all_gather(part, axis), shard)]
    all_gather x1 -> x0, blocking collectives: 22.4 us -> none  [entering(): everything = jax.tree.map(lambda part: lax.all_gather(part, axis), shard)]
    pallas_call x0 -> x1, Pallas kernels: none -> 18.7 us  [body(): pl.pallas_call(functools.partial(kernel, n, heads, groups), out_shape=(ja...]
    dynamic_slice x8 -> x0, local copies, waits for them, and re-layouts: 7.58 us -> none  [hop(): new = combine(before, jax.tree.map(lambda part: part[k], everything))]
    dot_general x3 -> x0, matrix products: 2.27 us -> none  [the longest x1 1.01 us: body(): jnp.einsum('shi,shj->ihj', keys_decayed, value_split, preferred_element_t...]
    select_n x9 -> x0, other arithmetic: 2.09 us -> none  [the longest x8 1.97 us: hop(): return jax.tree.map(lambda a, b: jnp.where(reached, a, b), new, before)]
    unnamed x10 -> x4, local copies, waits for them, and re-layouts: 3.56 us -> 2.32 us
  transfers between devices with their start and end apart: 2 -> 0, of which waited for: 2 -> 0; matrix products, arithmetic and copies ran while one was open for 10% -> 0% of each run, Pallas kernels for 0% -> 0%
where the time goes in v1:
time: 23.2 us; the launch traced here: 23 us
  Pallas kernels  18.7 us (81%)
  local copies, waits for them, and re-layouts  3.57 us (15%)
  between operations  0.65 us (3%)
    pallas_call x1, Pallas kernels, body(): pl.pallas_call(functools.partial(kernel, n, heads, groups), out_shape=(ja...  18.7 us
    unnamed x4, local copies, waits for them, and re-layouts  2.32 us
    reshape x1, local copies, waits for them, and re-layouts, body(): norm_gain.reshape(1, width)  1.25 us

profile of v1, /device:TPU:0, one launch (start us, length us, event | category | flops | bytes accessed | tf_op | source)
XLA Modules:
  0.0 23.0 jit_solution(17138154565822839261)
XLA Ops:
  0.6 1.2 %reshape.7.gain_ref = f32[1,384]{1,0:T(1,128)} reshape(f32[384]{0:T(512)} %param.9) | data formatting | bytes 3072 | tf_op jit(solution)/shard_map/reshape | solution.py:192
  1.9 18.7 %retention.1 = (bf16[384,384]{1,0:T(8,128)(2,1)}, f32[3,16,128]{2,1,0:T(8,128)}) custom-call(bf16[384,384]{1,0:T(8,128)(2,1)} %q_hbm.1, bf16[384,384]{1,0:T(8,128)(2,1)} %k_hbm.1, bf16[384,384]{1,0:T(8,128)(2,1)} %v_hbm.1, bf16[384,384]{1,0:T(8,128)(2,1)} %g_hbm.1, f32[1,384]{1,0:T(1,128)} %reshape.7.gain_ref), custom_call_target="tpu_custom_call" | custom-call | tf_op jit(solution)/shard_map/retention/pallas_call | solution.py:180
  20.6 0.0 copy-start
  20.6 1.7 %copy.9 = bf16[384,384]{1,0:T(8,128)(2,1)} copy(bf16[384,384]{1,0:T(8,128)(2,1)} %get-tuple-element.8) | data formatting | bytes 589824
  22.3 0.0 copy-done
  22.3 0.6 %copy.10 = f32[16,3,128]{2,0,1:T(8,128)} copy(f32[16,3,128]{2,0,1:T(8,128)S(1)} %bitcast.1) | data formatting | bytes 49152
Async XLA Ops:
  20.6 1.7 %copy-start = (f32[3,16,128]{2,1,0:T(8,128)S(1)}, f32[3,16,128]{2,1,0:T(8,128)}, u32[]{:S(2)}) copy-start(f32[3,16,128]{2,1,0:T(8,128)} %get-tuple-element.5) | copy-start | bytes 73732

commit v2 on v1

--- a/solution.py
+++ b/solution.py
@@ -106,8 +106,8 @@
             kd, v[:, cols(h)], (((0,), (0,)), ((), ())), preferred_element_type=jnp.float32
         )
         state[h] = local.reshape(n, rows, DH)
-    pl.semaphore_wait(barrier, n - 1)
-    for h in range(heads):
+        if h == 0:
+            pl.semaphore_wait(barrier, n - 1)
         send(state, got, me, (send1, recv1), h)
         got[h, me] = state[h, me]
 
@@ -128,7 +128,7 @@
     loads[3].wait()
     for h in range(heads):
         u = g[:, cols(h)].astype(jnp.float32)
-        gate[h] = u / (1.0 + jnp.exp(-u)) * gain_ref[:, cols(h)]
+        gate[h] = u / (1.0 + jnp.exp(-u)) * gain_ref[cols(h)][None, :]
 
     for h in range(heads):
         drain(got, recv1, h)
@@ -175,13 +175,13 @@
         slab = pltpu.VMEM((heads, n, rows, DH), jnp.float32)
         wide = pltpu.VMEM((tokens, width), jnp.bfloat16)
         tall = pltpu.VMEM((heads, tokens, DH), jnp.float32)
-        anywhere = pl.BlockSpec(memory_space=pl.ANY)
+        anywhere = pl.BlockSpec(memory_space=pltpu.HBM)
         vmem = pl.BlockSpec(memory_space=pltpu.VMEM)
         retained, final = pl.pallas_call(
             functools.partial(kernel, n, heads, groups),
             out_shape=(
-                jax.ShapeDtypeStruct((tokens, width), jnp.bfloat16),
-                jax.ShapeDtypeStruct((heads, rows, DH), jnp.float32),
+                pltpu.VMEM((tokens, width), jnp.bfloat16),
+                pltpu.VMEM((heads, rows, DH), jnp.float32),
             ),
             in_specs=[anywhere] * 4 + [vmem],
             out_specs=(vmem, vmem),
@@ -189,7 +189,7 @@
             + [pltpu.SemaphoreType.DMA((4,))] + [pltpu.SemaphoreType.DMA((heads,))] * 4,
             compiler_params=pltpu.CompilerParams(collective_id=0, has_side_effects=True),
             name="retention",
-        )(queries, key_rows, value_rows, gate_input, norm_gain.reshape(1, width))
+        )(queries, key_rows, value_rows, gate_input, norm_gain)
         return retained, final.transpose(1, 0, 2)
 
     return jax.shard_map(

time: 23.2 us -> 20.2 us (0.87)
  local copies, waits for them, and re-layouts: 3.57 us -> 1.32 us
  Pallas kernels: 18.7 us -> 18 us
    reshape x1 -> x0, local copies, waits for them, and re-layouts: 1.25 us -> none  [body(): norm_gain.reshape(1, width)]
    unnamed x4 -> x2, local copies, waits for them, and re-layouts: 2.32 us -> 1.32 us
    pallas_call x1, Pallas kernels: 18.7 us -> 18 us  [body(): pl.pallas_call(functools.partial(kernel, n, heads, groups), out_shape=(pl...]
where the time goes in v2:
time: 20.2 us; the launch traced here: 20 us
  Pallas kernels  18 us (89%)
  local copies, waits for them, and re-layouts  1.32 us (7%)
  between operations  0.64 us (3%)
    pallas_call x1, Pallas kernels, body(): pl.pallas_call(functools.partial(kernel, n, heads, groups), out_shape=(pl...  18 us
    unnamed x2, local copies, waits for them, and re-layouts  1.32 us

profile of v2, /device:TPU:0, one launch (start us, length us, event | category | flops | bytes accessed | tf_op | source)
XLA Modules:
  0.0 20.0 jit_solution(18278758656740480910)
XLA Ops:
  0.6 18.0 %retention.1 = (bf16[384,384]{1,0:T(8,128)(2,1)S(1)}, f32[3,16,128]{2,1,0:T(8,128)S(1)}) custom-call(bf16[384,384]{1,0:T(8,128)(2,1)} %q_hbm.1, bf16[384,384]{1,0:T(8,128)(2,1)} %k_hbm.1, bf16[384,384]{1,0:T(8,128)(2,1)} %v_hbm.1, bf16[384,384]{1,0:T(8,128)(2,1)} %g_hbm.1, f32[384]{0:T(512)} %gain_ref.1), custom_call_target="tpu_custom_call" | custom-call | tf_op jit(solution)/shard_map/retention/pallas_call | solution.py:180
  18.7 0.7 %copy.9 = bf16[384,384]{1,0:T(8,128)(2,1)} copy(bf16[384,384]{1,0:T(8,128)(2,1)S(1)} %get-tuple-element.6) | data formatting | bytes 589824
  19.4 0.6 %copy.10 = f32[16,3,128]{2,0,1:T(8,128)} copy(f32[16,3,128]{2,0,1:T(8,128)S(1)} %bitcast.1) | data formatting | bytes 49152

commit v3 on v2

--- a/solution.py
+++ b/solution.py
@@ -162,6 +162,17 @@
     for h in range(heads):
         drain(state, send1, h)
         drain(before, send2, h)
+
+
+def settle(res, fin, out_hbm, fin_hbm, sems):
+    copies = [
+        pltpu.make_async_copy(res, out_hbm, sems.at[0]),
+        pltpu.make_async_copy(fin, fin_hbm, sems.at[1]),
+    ]
+    for copy in copies:
+        copy.start()
+    for copy in copies:
+        copy.wait()
 
 
 def solution(mesh):
@@ -190,6 +201,18 @@
             compiler_params=pltpu.CompilerParams(collective_id=0, has_side_effects=True),
             name="retention",
         )(queries, key_rows, value_rows, gate_input, norm_gain)
+        retained, final = pl.pallas_call(
+            settle,
+            out_shape=(
+                jax.ShapeDtypeStruct((tokens, width), jnp.bfloat16),
+                jax.ShapeDtypeStruct((heads, rows, DH), jnp.float32),
+            ),
+            in_specs=[vmem] * 2,
+            out_specs=(anywhere, anywhere),
+            scratch_shapes=[pltpu.SemaphoreType.DMA((2,))],
+            compiler_params=pltpu.CompilerParams(vmem_limit_bytes=1 << 20, has_side_effects=True),
+            name="settle",
+        )(retained, final)
         return retained, final.transpose(1, 0, 2)
 
     return jax.shard_map(

time: 20.2 us -> 19.6 us (0.970)
  local copies, waits for them, and re-layouts: 1.32 us -> 0 us
  Pallas kernels: 18 us -> 18.8 us
    unnamed x2 -> x0, local copies, waits for them, and re-layouts: 1.32 us -> none
    pallas_call x0 -> x1, Pallas kernels: none -> 0.74 us  [body(): pl.pallas_call(settle, out_shape=(jax.ShapeDtypeStruct((tokens, width), j...]
where the time goes in v3:
time: 19.6 us; the launch traced here: 19.4 us
  Pallas kernels  18.8 us (96%)
  between operations  0.64 us (3%)
    pallas_call x1, Pallas kernels, body(): pl.pallas_call(functools.partial(kernel, n, heads, groups), out_shape=(pl...  18 us
    pallas_call x1, Pallas kernels, body(): pl.pallas_call(settle, out_shape=(jax.ShapeDtypeStruct((tokens, width), j...  0.74 us

profile of v3, /device:TPU:0, one launch (start us, length us, event | category | flops | bytes accessed | tf_op | source)
XLA Modules:
  0.0 19.4 jit_solution(15623073843801388079)
XLA Ops:
  0.6 18.0 %retention.1 = (bf16[384,384]{1,0:T(8,128)(2,1)S(1)}, f32[3,16,128]{2,1,0:T(8,128)S(1)}) custom-call(bf16[384,384]{1,0:T(8,128)(2,1)} %q_hbm.1, bf16[384,384]{1,0:T(8,128)(2,1)} %k_hbm.1, bf16[384,384]{1,0:T(8,128)(2,1)} %v_hbm.1, bf16[384,384]{1,0:T(8,128)(2,1)} %g_hbm.1, f32[384]{0:T(512)} %gain_ref.1), custom_call_target="tpu_custom_call" | custom-call | tf_op jit(solution)/shard_map/retention/pallas_call | solution.py:191
  18.7 0.7 %settle.1 = (bf16[384,384]{1,0:T(8,128)(2,1)}, f32[3,16,128]{2,1,0:T(8,128)}) custom-call(bf16[384,384]{1,0:T(8,128)(2,1)S(1)} %get-tuple-element.6.res, f32[3,16,128]{2,1,0:T(8,128)S(1)} %get-tuple-element.7.fin), custom_call_target="tpu_custom_call" | custom-call | tf_op jit(solution)/shard_map/settle/pallas_call | solution.py:204

commit v4 on v3

--- a/solution.py
+++ b/solution.py
@@ -80,13 +80,13 @@
     def cols(h):
         return slice(h * DH, (h + 1) * DH)
 
-    def send(source, target, slot_of, sems, h):
+    def send(source, target, sems):
         def act(peer):
             pltpu.make_async_remote_copy(
-                src_ref=source.at[h, peer],
-                dst_ref=target.at[h, me],
-                send_sem=sems[0].at[h],
-                recv_sem=sems[1].at[h],
+                src_ref=source.at[peer],
+                dst_ref=target.at[me],
+                send_sem=sems[0].at[0],
+                recv_sem=sems[1].at[0],
                 device_id={"seq": peer},
                 device_id_type=MESH,
             ).start()
@@ -94,8 +94,8 @@
         each_peer(me, n, act)
 
     def drain(buffer, sem, h):
-        piece = buffer.at[h, pl.ds(0, n - 1)]
-        pltpu.make_async_copy(piece, piece, sem.at[h]).wait()
+        piece = buffer.at[pl.ds(0, n - 1)]
+        pltpu.make_async_copy(piece, piece, sem.at[0]).wait()
 
     loads[0].wait()
     loads[1].wait()
@@ -105,11 +105,12 @@
         local = lax.dot_general(
             kd, v[:, cols(h)], (((0,), (0,)), ((), ())), preferred_element_type=jnp.float32
         )
-        state[h] = local.reshape(n, rows, DH)
+        state[:, h] = local.reshape(n, rows, DH)
         if h == 0:
             pl.semaphore_wait(barrier, n - 1)
-        send(state, got, me, (send1, recv1), h)
-        got[h, me] = state[h, me]
+        if h == heads - 1:
+            send(state, got, (send1, recv1))
+            got[me] = state[me]
 
     loads[2].wait()
     offsets = (
@@ -131,12 +132,13 @@
         gate[h] = u / (1.0 + jnp.exp(-u)) * gain_ref[cols(h)][None, :]
 
     for h in range(heads):
-        drain(got, recv1, h)
+        if h == 0:
+            drain(got, recv1, h)
         block_decay = jnp.exp(jnp.full((rows, DH), tokens, jnp.float32) * logs[h])
 
         def hop(b, total):
-            before[h, b] = total
-            return block_decay * total + got[h, b]
+            before[b, h] = total
+            return block_decay * total + got[b, h]
 
         total = jnp.zeros((rows, DH), jnp.float32)
         if n <= 16:
@@ -144,14 +146,16 @@
                 total = hop(b, total)
         else:
             total = lax.fori_loop(0, n, hop, total)
-        send(before, carried, me, (send2, recv2), h)
-        carried[h, me] = before[h, me]
+        if h == heads - 1:
+            send(before, carried, (send2, recv2))
+            carried[me] = before[me]
         fin_ref[h] = total
 
     for h in range(heads):
         lead = jnp.exp((place + 1.0) * logs[h])
-        drain(carried, recv2, h)
-        low = carried[h].reshape(DH, DH).astype(jnp.bfloat16)
+        if h == 0:
+            drain(carried, recv2, h)
+        low = carried[:, h].reshape(DH, DH).astype(jnp.bfloat16)
         outer = jnp.dot(q[:, cols(h)], low, preferred_element_type=jnp.float32)
         mixture = inner[h] + outer * lead
         centred = mixture - jnp.mean(mixture, axis=-1, keepdims=True)
@@ -159,9 +163,8 @@
         normed = centred * lax.rsqrt(variance + 1e-05)
         out_ref[:, cols(h)] = (normed * gate[h]).astype(jnp.bfloat16)
 
-    for h in range(heads):
-        drain(state, send1, h)
-        drain(before, send2, h)
+    drain(state, send1, 0)
+    drain(before, send2, 0)
 
 
 def settle(res, fin, out_hbm, fin_hbm, sems):
@@ -183,7 +186,7 @@
         tokens, width = queries.shape
         heads = width // DH
         rows = DH // n
-        slab = pltpu.VMEM((heads, n, rows, DH), jnp.float32)
+        slab = pltpu.VMEM((n, heads, rows, DH), jnp.float32)
         wide = pltpu.VMEM((tokens, width), jnp.bfloat16)
         tall = pltpu.VMEM((heads, tokens, DH), jnp.float32)
         anywhere = pl.BlockSpec(memory_space=pltpu.HBM)

time: 19.6 us -> 19.4 us (0.990)
  Pallas kernels: 18.8 us -> 18.6 us
    pallas_call x1, Pallas kernels: 18 us -> 17.8 us  [body(): pl.pallas_call(functools.partial(kernel, n, heads, groups), out_shape=(pl...]
where the time goes in v4:
time: 19.4 us; the launch traced here: 19.2 us
  Pallas kernels  18.6 us (96%)
  between operations  0.64 us (3%)
    pallas_call x1, Pallas kernels, body(): pl.pallas_call(functools.partial(kernel, n, heads, groups), out_shape=(pl...  17.8 us
    pallas_call x1, Pallas kernels, body(): pl.pallas_call(settle, out_shape=(jax.ShapeDtypeStruct((tokens, width), j...  0.74 us

profile of v4, /device:TPU:0, one launch (start us, length us, event | category | flops | bytes accessed | tf_op | source)
XLA Modules:
  0.0 19.2 jit_solution(10347466596223069050)
XLA Ops:
  0.6 17.8 %retention.1 = (bf16[384,384]{1,0:T(8,128)(2,1)S(1)}, f32[3,16,128]{2,1,0:T(8,128)S(1)}) custom-call(bf16[384,384]{1,0:T(8,128)(2,1)} %q_hbm.1, bf16[384,384]{1,0:T(8,128)(2,1)} %k_hbm.1, bf16[384,384]{1,0:T(8,128)(2,1)} %v_hbm.1, bf16[384,384]{1,0:T(8,128)(2,1)} %g_hbm.1, f32[384]{0:T(512)} %gain_ref.1), custom_call_target="tpu_custom_call" | custom-call | tf_op jit(solution)/shard_map/retention/pallas_call | solution.py:194
  18.5 0.7 %settle.1 = (bf16[384,384]{1,0:T(8,128)(2,1)}, f32[3,16,128]{2,1,0:T(8,128)}) custom-call(bf16[384,384]{1,0:T(8,128)(2,1)S(1)} %get-tuple-element.6.res, f32[3,16,128]{2,1,0:T(8,128)S(1)} %get-tuple-element.7.fin), custom_call_target="tpu_custom_call" | custom-call | tf_op jit(solution)/shard_map/settle/pallas_call | solution.py:207
